TPU v7x, 32 devices: a whole 2x2x4 slice. The times are simulated.
32 devices in a mesh: wide: 8 (over y, x, core), narrow: 4 (over z).
Axes of the slice: x: 2, y: 2, z: 4, core: 2. Of those that a mesh axis runs over, the one named last changes fastest.
Arguments:
- tokens: bfloat16 [16, 1184, 1024], P('wide', 'narrow'), may hold values from -6 to 6
- timestep: bfloat16 [16, 1024], P('wide'), may hold values from -6 to 6
- context: int32 [16, 2], P('wide'), may hold values from 0 to 475
- w_qkv: bfloat16 [1024, 3, 1024], P('wide', None, 'narrow'), may hold values from -0.1875 to 0.1875
- w_out: bfloat16 [1024, 1024], P('narrow', 'wide'), may hold values from -1.5 to 1.5
- w_up: bfloat16 [1024, 4096], P('wide', 'narrow'), may hold values from -0.1875 to 0.1875
- w_down: bfloat16 [4096, 1024], P('narrow', 'wide'), may hold values from -0.09375 to 0.09375
- b_up: bfloat16 [4096], P(('wide', 'narrow')), may hold values from -3 to 3
- biases: bfloat16 [6, 1024], P(None, ('wide', 'narrow')), may hold values from -3 to 3
- gains: bfloat16 [2, 1024], P(None, ('wide', 'narrow')), may hold values from 0.25 to 1.75
- cotangent: bfloat16 [16, 1184, 1024], P('wide', 'narrow'), may hold values from -6 to 6
Outputs:
- output: bfloat16 [16, 1184, 1024], P('wide', 'narrow')
- grad_tokens: float32 [16, 1184, 1024], P('wide', 'narrow')
- grad_qkv: float32 [1024, 3, 1024], P('wide', None, 'narrow')
- grad_out: float32 [1024, 1024], P('narrow', 'wide')
- grad_up: float32 [1024, 4096], P('wide', 'narrow')
- grad_down: float32 [4096, 1024], P('narrow', 'wide')
- grad_b_up: float32 [4096], P(('wide', 'narrow'))
- grad_biases: float32 [6, 1024], P(None, ('wide', 'narrow'))
- grad_gains: float32 [2, 1024], P(None, ('wide', 'narrow'))
All inputs are finite; a program needn't handle non-finite values.
Results may differ from a plain program's by a relative error of at most 0.018.
Values may be sent and summed in bfloat16 or wider, within the bound.
A program may use at most 256 MiB of HBM per device.

v0:
```python
from functools import partial

import jax
import jax.numpy as jnp
from jax import lax
from jax.sharding import PartitionSpec as P

HEAD_DIM = 64
ITEM = 592
NOISE = 25
MB = 2


def spread_rows(piece):
    return lax.all_gather(piece, "narrow", axis=1, tiled=True)


def collect_sums(term):
    return lax.psum_scatter(
        term.astype(jnp.bfloat16), "narrow", scatter_dimension=1, tiled=True
    ).astype(jnp.float32)


def fetch_weights(w_qkv, w_out, w_up, w_down):
    full_qkv, full_out, full_up, full_down = (
        lax.all_gather(w_qkv, "wide", axis=0, tiled=True),
        lax.all_gather(w_out, "wide", axis=1, tiled=True),
        lax.all_gather(w_up, "wide", axis=0, tiled=True),
        lax.all_gather(w_down, "wide", axis=1, tiled=True),
    )
    whole_qkv, whole_out = (
        lax.all_gather(full_qkv, "narrow", axis=2, tiled=True),
        lax.all_gather(full_out, "narrow", axis=0, tiled=True),
    )
    return (whole_qkv, whole_out, full_up, full_down)


def reduce_grads(grad_set):
    return (
        lax.psum_scatter(
            grad_set[0].astype(jnp.bfloat16), "wide", scatter_dimension=0, tiled=True
        ).astype(jnp.float32),
        lax.psum_scatter(
            grad_set[1].astype(jnp.bfloat16), "wide", scatter_dimension=1, tiled=True
        ).astype(jnp.float32),
        lax.psum_scatter(
            grad_set[2].astype(jnp.bfloat16), "wide", scatter_dimension=0, tiled=True
        ).astype(jnp.float32),
        lax.psum_scatter(
            grad_set[3].astype(jnp.bfloat16), "wide", scatter_dimension=1, tiled=True
        ).astype(jnp.float32),
    )


def norm_forward(hidden, gain_vec, shift_vec):
    center = hidden - jnp.mean(hidden, -1, keepdims=True)
    inverse = lax.rsqrt(jnp.mean(center * center, -1, keepdims=True) + 1e-05)
    normed = center * inverse
    return (normed * gain_vec + shift_vec, normed, inverse)


def norm_backward(upstream, normed, inverse, gain_vec):
    scaled = upstream * gain_vec
    return inverse * (
        scaled
        - jnp.mean(scaled, -1, keepdims=True)
        - normed * jnp.mean(scaled * normed, -1, keepdims=True)
    )


def masked_scores(queries, key_rows, key_valid):
    scores = jnp.einsum("qhe,khe->hqk", queries, key_rows, preferred_element_type=jnp.float32)
    scores = scores * queries.shape[-1] ** (-0.5)
    item_index = jnp.arange(queries.shape[0], dtype=jnp.int32) // ITEM
    allowed = (item_index[:, None] == item_index[None, :]) & key_valid[None, :]
    return jnp.where(allowed[None, :, :], scores, -jnp.inf)


def attend_row(inputs):
    queries, key_rows, value_rows, key_valid = inputs
    scores = masked_scores(queries, key_rows, key_valid)
    top_score = jnp.max(scores, -1, keepdims=True)
    log_total = top_score + jnp.log(jnp.sum(jnp.exp(scores - top_score), -1, keepdims=True))
    probs_low = jnp.exp(scores - log_total).astype(jnp.bfloat16)
    attended = jnp.einsum("hqk,khe->qhe", probs_low, value_rows, preferred_element_type=jnp.float32)
    return (attended.reshape(attended.shape[0], -1).astype(jnp.bfloat16), log_total)


def attend_back(inputs):
    queries, key_rows, value_rows, key_valid, log_total, d_att = inputs
    probs = jnp.exp(masked_scores(queries, key_rows, key_valid) - log_total)
    probs_low = probs.astype(jnp.bfloat16)
    d_prob = jnp.einsum("qhe,khe->hqk", d_att, value_rows, preferred_element_type=jnp.float32)
    d_score = probs * (d_prob - jnp.sum(probs * d_prob, -1, keepdims=True))
    d_score_low = d_score.astype(jnp.bfloat16)
    factor = queries.shape[-1] ** (-0.5)
    d_queries = (
        jnp.einsum("hqk,khe->qhe", d_score_low, key_rows, preferred_element_type=jnp.float32)
        * factor
    )
    d_keys = (
        jnp.einsum("hqk,qhe->khe", d_score_low, queries, preferred_element_type=jnp.float32)
        * factor
    )
    d_values = jnp.einsum("hqk,qhe->khe", probs_low, d_att, preferred_element_type=jnp.float32)
    return (d_queries, d_keys, d_values)


def shards(tokens, timestep, context, w_qkv, w_out, w_up, w_down, b_up, biases, gains, cotangent):
    narrow_count = lax.axis_size("narrow")
    narrow_index = lax.axis_index("narrow")
    rows_here, piece_len, model_width = tokens.shape
    seq_len = piece_len * narrow_count
    local_width = w_qkv.shape[2]
    local_hidden = w_up.shape[1]
    heads_here = local_width // HEAD_DIM
    batch_rows = rows_here // MB
    bias_all, gain_all, up_bias_all = (
        lax.all_gather(biases, ("wide", "narrow"), axis=1, tiled=True),
        lax.all_gather(gains, ("wide", "narrow"), axis=1, tiled=True),
        lax.all_gather(b_up, ("wide", "narrow"), axis=0, tiled=True),
    )
    bias_all = bias_all.astype(jnp.float32)
    gain_all = gain_all.astype(jnp.float32)
    up_bias_all = up_bias_all.astype(jnp.float32)
    query_bias = lax.dynamic_slice_in_dim(bias_all[0], narrow_index * local_width, local_width)
    value_bias = lax.dynamic_slice_in_dim(bias_all[1], narrow_index * local_width, local_width)
    up_bias = lax.dynamic_slice_in_dim(up_bias_all, narrow_index * local_hidden, local_hidden)
    position = jnp.arange(seq_len, dtype=jnp.int32)
    item_index = position // ITEM
    offset = position - item_index * ITEM
    item_start = jnp.where(item_index[None, :] == 0, context[:, 0:1], context[:, 1:2])
    noisy_mask = (offset[None, :] >= item_start) & (offset[None, :] < item_start + NOISE)
    key_valid = offset[None, :] < item_start + NOISE
    noisy_here = lax.dynamic_slice_in_dim(noisy_mask, narrow_index * piece_len, piece_len, 1)
    grad_shares = None
    zero_width = jnp.zeros((model_width,), jnp.float32)
    sum_query_bias = jnp.zeros((local_width,), jnp.float32)
    sum_value_bias = jnp.zeros((local_width,), jnp.float32)
    sum_up_bias = jnp.zeros(up_bias.shape, jnp.float32)
    sum_out_bias = zero_width
    sum_down_bias = zero_width
    sum_shift_one = zero_width
    sum_shift_two = zero_width
    sum_gain_one = zero_width
    sum_gain_two = zero_width
    output_parts = []
    grad_parts = []
    head_shape = (batch_rows, seq_len, heads_here, HEAD_DIM)
    for batch in range(MB):
        row_range = slice(batch * batch_rows, (batch + 1) * batch_rows)
        token_part = tokens[row_range].astype(jnp.float32)
        embed_part = timestep[row_range].astype(jnp.float32)
        valid_part = key_valid[row_range]
        x_here = token_part + jnp.where(
            noisy_here[row_range][:, :, None], embed_part[:, None, :], 0.0
        )
        whole_qkv, whole_out, full_up, full_down = fetch_weights(w_qkv, w_out, w_up, w_down)
        local_qkv = lax.dynamic_slice_in_dim(whole_qkv, narrow_index * local_width, local_width, 2)
        local_out = lax.dynamic_slice_in_dim(whole_out, narrow_index * local_width, local_width, 0)
        x_all = spread_rows(x_here.astype(jnp.bfloat16))
        projected = jnp.einsum(
            "rsd,dcf->crsf", x_all, local_qkv, preferred_element_type=jnp.float32
        )
        queries = (projected[0] + query_bias).astype(jnp.bfloat16).reshape(head_shape)
        key_rows = projected[1].astype(jnp.bfloat16).reshape(head_shape)
        value_rows = (projected[2] + value_bias).astype(jnp.bfloat16).reshape(head_shape)
        attended, log_total = lax.map(attend_row, (queries, key_rows, value_rows, valid_part))
        attended_here = lax.all_to_all(attended, "narrow", split_axis=1, concat_axis=2, tiled=True)
        first_sum = (
            x_here
            + jnp.einsum(
                "rsf,fd->rsd", attended_here, whole_out, preferred_element_type=jnp.float32
            )
            + bias_all[2]
        )
        first_norm, normed_one, inverse_one = norm_forward(first_sum, gain_all[0], bias_all[4])
        ffn_input = spread_rows(first_norm.astype(jnp.bfloat16))
        pre_act = (
            jnp.einsum("rsd,df->rsf", ffn_input, full_up, preferred_element_type=jnp.float32)
            + up_bias
        )
        activated, gelu_pull = jax.vjp(partial(jax.nn.gelu, approximate=False), pre_act)
        activated = activated.astype(jnp.bfloat16)
        down_term = jnp.einsum(
            "rsf,fd->rsd", activated, full_down, preferred_element_type=jnp.float32
        )
        second_sum = first_norm + collect_sums(down_term) + bias_all[3]
        result, normed_two, inverse_two = norm_forward(second_sum, gain_all[1], bias_all[5])
        output_parts.append(result.astype(jnp.bfloat16))
        cot_part = cotangent[row_range].astype(jnp.float32)
        sum_gain_two = sum_gain_two + jnp.sum(cot_part * normed_two, (0, 1))
        sum_shift_two = sum_shift_two + jnp.sum(cot_part, (0, 1))
        d_second = norm_backward(cot_part, normed_two, inverse_two, gain_all[1])
        sum_down_bias = sum_down_bias + jnp.sum(d_second, (0, 1))
        d_second_all = spread_rows(d_second.astype(jnp.bfloat16))
        grad_down = jnp.einsum(
            "rsf,rsd->fd", activated, d_second_all, preferred_element_type=jnp.float32
        )
        d_act = jnp.einsum(
            "rsd,fd->rsf", d_second_all, full_down, preferred_element_type=jnp.float32
        )
        d_pre = gelu_pull(d_act)[0]
        sum_up_bias = sum_up_bias + jnp.sum(d_pre, (0, 1))
        d_pre_low = d_pre.astype(jnp.bfloat16)
        grad_up = jnp.einsum(
            "rsd,rsf->df", ffn_input, d_pre_low, preferred_element_type=jnp.float32
        )
        back_term = jnp.einsum(
            "rsf,df->rsd", d_pre_low, full_up, preferred_element_type=jnp.float32
        )
        d_first_norm = d_second + collect_sums(back_term)
        sum_gain_one = sum_gain_one + jnp.sum(d_first_norm * normed_one, (0, 1))
        sum_shift_one = sum_shift_one + jnp.sum(d_first_norm, (0, 1))
        d_first = norm_backward(d_first_norm, normed_one, inverse_one, gain_all[0])
        sum_out_bias = sum_out_bias + jnp.sum(d_first, (0, 1))
        d_first_all = spread_rows(d_first.astype(jnp.bfloat16))
        grad_out = jnp.einsum(
            "rsf,rsd->fd", attended, d_first_all, preferred_element_type=jnp.float32
        )
        d_att = jnp.einsum(
            "rsd,fd->rsf", d_first_all, local_out, preferred_element_type=jnp.float32
        ).astype(jnp.bfloat16)
        d_queries, d_keys, d_values = lax.map(
            attend_back,
            (queries, key_rows, value_rows, valid_part, log_total, d_att.reshape(head_shape)),
        )
        flat_shape = (batch_rows, seq_len, local_width)
        d_queries = d_queries.reshape(flat_shape)
        d_keys = d_keys.reshape(flat_shape)
        d_values = d_values.reshape(flat_shape)
        sum_query_bias = sum_query_bias + jnp.sum(d_queries, (0, 1))
        sum_value_bias = sum_value_bias + jnp.sum(d_values, (0, 1))
        d_proj = jnp.stack([d_queries, d_keys, d_values]).astype(jnp.bfloat16)
        grad_qkv = jnp.einsum("rsd,crsf->dcf", x_all, d_proj, preferred_element_type=jnp.float32)
        d_proj_here = lax.all_to_all(d_proj, "narrow", split_axis=2, concat_axis=3, tiled=True)
        grad_parts.append(
            d_first
            + jnp.einsum(
                "crsf,dcf->rsd", d_proj_here, whole_qkv, preferred_element_type=jnp.float32
            )
        )
        grad_set = (grad_qkv, grad_out, grad_up, grad_down)
        shares = reduce_grads(grad_set)
        grad_shares = (
            shares
            if grad_shares is None
            else tuple((left + right for left, right in zip(grad_shares, shares)))
        )
    placed_query = lax.dynamic_update_slice_in_dim(
        zero_width, sum_query_bias, narrow_index * local_width, 0
    )
    placed_value = lax.dynamic_update_slice_in_dim(
        zero_width, sum_value_bias, narrow_index * local_width, 0
    )
    placed_up = lax.dynamic_update_slice_in_dim(
        jnp.zeros(up_bias_all.shape, jnp.float32), sum_up_bias, narrow_index * local_hidden, 0
    )
    bias_terms = jnp.stack(
        [placed_query, placed_value, sum_out_bias, sum_down_bias, sum_shift_one, sum_shift_two]
    )
    gain_terms = jnp.stack([sum_gain_one, sum_gain_two])
    grad_b_up, grad_biases, grad_gains = (
        lax.psum_scatter(placed_up, ("wide", "narrow"), scatter_dimension=0, tiled=True),
        lax.psum_scatter(bias_terms, ("wide", "narrow"), scatter_dimension=1, tiled=True),
        lax.psum_scatter(gain_terms, ("wide", "narrow"), scatter_dimension=1, tiled=True),
    )
    output = jnp.concatenate(output_parts, 0)
    grad_tokens = jnp.concatenate(grad_parts, 0)
    return (
        output,
        grad_tokens,
        grad_shares[0],
        grad_shares[1],
        grad_shares[2],
        grad_shares[3],
        grad_b_up,
        grad_biases,
        grad_gains,
    )


def solution(mesh):
    placed = (
        P("wide", "narrow", None),
        P("wide", None),
        P("wide", None),
        P("wide", None, "narrow"),
        P("narrow", "wide"),
        P("wide", "narrow"),
        P("narrow", "wide"),
        P(("wide", "narrow")),
        P(None, ("wide", "narrow")),
        P(None, ("wide", "narrow")),
        P("wide", "narrow", None),
    )
    return jax.shard_map(
        shards,
        mesh=mesh,
        in_specs=placed,
        out_specs=(
            P("wide", "narrow", None),
            P("wide", "narrow", None),
            P("wide", None, "narrow"),
            P("narrow", "wide"),
            P("wide", "narrow"),
            P("narrow", "wide"),
            P(("wide", "narrow")),
            P(None, ("wide", "narrow")),
            P(None, ("wide", "narrow")),
        ),
        check_vma=False,
    )
```

profile of v0, /device:TPU:0, one launch (start us, length us, event | category | flops | bytes accessed | tf_op | source)
XLA Modules:
  0.0 1660.6 jit_solution(4746009035871325218)
XLA Ops:
  12.8 25.4 %all-gather.17.cloned.1.call-done = bf16[1024,3,256]{2,0,1:T(8,128)(2,1)} async-done(((bf16[128,3,256]{2,0,1:T(8,128)(2,1)}), bf16[1024,3,256]{2,0,1:T(8,128)(2,1)}) %all-gather.17.cloned.1.call-update) | async-done | bytes 1572880 | tf_op jit(solution)/shard_map/all_gather | solution.py:26
  38.9 10.9 all_gather.61
  50.5 77.5 %all-gather = bf16[32,32,6]{1,2,0:T(8,128)(2,1)S(1)} all-gather(bf16[1,32,6]{1,2,0:T(8,128)(2,1)S(1)} %bitcast.340), channel_id=1, replica_groups=mesh['wide'=8,'narrow'=4] {'wide','narrow'}, dimensions={0}, use_global_device_ids=true | all-gather | bytes 12672 | tf_op jit(solution)/shard_map/all_gather | solution.py:119
  132.1 75.0 %all-gather.19.cloned.1.call-done = bf16[1024,3,1024]{2,0,1:T(8,128)(2,1)} async-done(((bf16[1024,3,256]{2,0,1:T(8,128)(2,1)}), bf16[1024,3,1024]{2,0,1:T(8,128)(2,1)}) %all-gather.19.cloned.1.call-update) | async-done | bytes 6291472 | tf_op jit(solution)/shard_map/all_gather | solution.py:32
  207.2 4.2 convolution_bitcast_fusion
  212.6 46.0 %all-gather.21.cloned.1.call-done = bf16[1,1184,1024]{2,1,0:T(8,128)(2,1)} async-done(((bf16[1,296,1024]{2,1,0:T(8,128)(2,1)}), bf16[1,1184,1024]{2,1,0:T(8,128)(2,1)}) %all-gather.21.cloned.1.call-update) | async-done | bytes 2424848 | tf_op jit(solution)/shard_map/all_gather | solution.py:15
  258.6 4.2 convolution_bitcast_fusion.1
  276.2 12.2 fusion.177
  288.4 10.6 exponential_reduce_fusion.1
  299.0 11.7 fusion.36
  313.5 8.3 reduce.48
  324.4 4.3 all-to-all-start
  328.7 11.9 fusion.179
  340.6 10.1 exponential_reduce_fusion
  350.7 11.7 fusion.39
  364.9 6.4 reduce.49
  372.3 5.0 all-to-all-start.1
  377.3 72.9 %all-gather.1 = bf16[32,32,2]{1,2,0:T(2,128)(2,1)S(1)} all-gather(bf16[1,32,2]{1,2,0:T(2,128)(2,1)S(1)} %bitcast.341), channel_id=1, replica_groups=mesh['wide'=8,'narrow'=4] {'wide','narrow'}, dimensions={0}, use_global_device_ids=true | all-gather | bytes 4224 | tf_op jit(solution)/shard_map/all_gather | solution.py:120
  461.7 65.3 %all-gather.2 = bf16[32,1,128]{2,1,0:T(2,128)(2,1)S(1)} all-gather(bf16[1,1,128]{2,1,0:T(2,128)(2,1)S(1)} %bitcast.342), channel_id=1, replica_groups=mesh['wide'=8,'narrow'=4] {'wide','narrow'}, dimensions={0}, use_global_device_ids=true | all-gather | bytes 8448 | tf_op jit(solution)/shard_map/all_gather | solution.py:121
  527.2 16.8 %multiply_convert_fusion.2 = (bf16[1184,1024]{1,0:T(8,128)(2,1)}, f32[1184,1024]{1,0:T(8,128)}, f32[1184,1024]{1,0:T(8,128)}) fusion(f32[1024]{0:T(1024)S(1)} %dynamic_slice.67, bf16[1024,1024]{1,0:T(8,128)(2,1)} %all-gather.27.cloned.1.call-done, bf16[1,1184,1024]{2,1,0:T(8,128)(2,1)} %all-gather.33.cloned.1.call-done), kind=kOutput, calls=%fused_computation.22 | convolution fusion | flops 2563047424 | bytes 16650240 | tf_op jit(solution)/shard_map/rsd,df->rsf/dot_general | solution.py:180
  543.9 6.5 fusion.17
  550.5 41.4 %all-gather.25.cloned.1.call-done = bf16[1,1184,1024]{2,1,0:T(8,128)(2,1)} async-done(((bf16[1,296,1024]{2,1,0:T(8,128)(2,1)}), bf16[1,1184,1024]{2,1,0:T(8,128)(2,1)}) %all-gather.25.cloned.1.call-update) | async-done | bytes 2424848 | tf_op jit(solution)/shard_map/all_gather | solution.py:15
  591.9 17.0 %multiply_convert_fusion.3 = (bf16[1184,1024]{1,0:T(8,128)(2,1)S(1)}, f32[1184,1024]{1,0:T(8,128)}, f32[1184,1024]{1,0:T(8,128)}) fusion(f32[1024]{0:T(1024)S(1)} %dynamic_slice.67, bf16[1024,1024]{1,0:T(8,128)(2,1)} %all-gather.27.cloned.1.call-done, bf16[1,1184,1024]{2,1,0:T(8,128)(2,1)} %all-gather.25.cloned.1.call-done), kind=kOutput, calls=%fused_computation.35 | convolution fusion | flops 2563047424 | bytes 16650240 | tf_op jit(solution)/shard_map/rsd,df->rsf/dot_general | solution.py:180
  614.4 27.4 %reduce-scatter.29.cloned.1.call-done = bf16[1,296,1024]{2,1,0:T(8,128)(2,1)} async-done(((bf16[1,1184,1024]{2,1,0:T(8,128)(2,1)}), bf16[1,296,1024]{2,1,0:T(8,128)(2,1)}) %reduce-scatter.29.cloned.1.call-update) | async-done | bytes 606224 | tf_op jit(solution)/shard_map/reduce_scatter | solution.py:19
  641.7 51.4 %reduce-scatter.27.cloned.1.call-done = bf16[1,296,1024]{2,1,0:T(8,128)(2,1)} async-done(((bf16[1,1184,1024]{2,1,0:T(8,128)(2,1)}), bf16[1,296,1024]{2,1,0:T(8,128)(2,1)}) %reduce-scatter.27.cloned.1.call-update) | async-done | bytes 606224 | tf_op jit(solution)/shard_map/reduce_scatter | solution.py:19
  701.6 49.8 %all-gather.35.cloned.1.call-done = bf16[1,1184,1024]{2,1,0:T(8,128)(2,1)} async-done(((bf16[1,296,1024]{2,1,0:T(8,128)(2,1)}), bf16[1,1184,1024]{2,1,0:T(8,128)(2,1)}) %all-gather.35.cloned.1.call-update) | async-done | bytes 2424848 | tf_op jit(solution)/shard_map/all_gather | solution.py:15
  751.4 10.1 fusion.181
  762.9 4.0 fusion.18
  767.0 35.9 %all-gather.39.cloned.1.call-done = bf16[1,1184,1024]{2,1,0:T(8,128)(2,1)} async-done(((bf16[1,296,1024]{2,1,0:T(8,128)(2,1)}), bf16[1,1184,1024]{2,1,0:T(8,128)(2,1)}) %all-gather.39.cloned.1.call-update) | async-done | bytes 2424848 | tf_op jit(solution)/shard_map/all_gather | solution.py:15
  802.9 10.0 fusion.182
  814.4 4.1 fusion.19
  818.9 34.4 %reduce-scatter.31.cloned.1.call-done = bf16[1,296,1024]{2,1,0:T(8,128)(2,1)} async-done(((bf16[1,1184,1024]{2,1,0:T(8,128)(2,1)}), bf16[1,296,1024]{2,1,0:T(8,128)(2,1)}) %reduce-scatter.31.cloned.1.call-update) | async-done | bytes 606224 | tf_op jit(solution)/shard_map/reduce_scatter | solution.py:19
  855.5 48.4 %reduce-scatter.33.cloned.1.call-done = bf16[1,296,1024]{2,1,0:T(8,128)(2,1)} async-done(((bf16[1,1184,1024]{2,1,0:T(8,128)(2,1)}), bf16[1,296,1024]{2,1,0:T(8,128)(2,1)}) %reduce-scatter.33.cloned.1.call-update) | async-done | bytes 606224 | tf_op jit(solution)/shard_map/reduce_scatter | solution.py:19
  911.4 5.3 fusion.83
  919.5 5.3 fusion.80
  927.5 6.8 fusion.77
  934.4 5.8 fusion.74
  941.5 19.7 %all-gather.41.cloned.1.call-done = bf16[1,1184,1024]{2,1,0:T(8,128)(2,1)} async-done(((bf16[1,296,1024]{2,1,0:T(8,128)(2,1)}), bf16[1,1184,1024]{2,1,0:T(8,128)(2,1)}) %all-gather.41.cloned.1.call-update) | async-done | bytes 2424848 | tf_op jit(solution)/shard_map/all_gather | solution.py:15
  964.1 11.8 fusion.171
  975.9 15.2 multiply_reduce_fusion
  991.0 22.0 %all-gather.37.cloned.1.call-done = bf16[1,1184,1024]{2,1,0:T(8,128)(2,1)} async-done(((bf16[1,296,1024]{2,1,0:T(8,128)(2,1)}), bf16[1,1184,1024]{2,1,0:T(8,128)(2,1)}) %all-gather.37.cloned.1.call-update) | async-done | bytes 2424848 | tf_op jit(solution)/shard_map/all_gather | solution.py:15
  1016.0 10.7 fusion.172
  1026.7 15.2 multiply_reduce_fusion.1
  1042.0 22.4 %multiply_convert_fusion = bf16[4,1184,1184]{1,2,0:T(8,128)(2,1)} fusion(f32[4,1184,1184]{1,2,0:T(8,128)} %get-tuple-element.205, f32[4,1184,1184]{1,2,0:T(8,128)} %get-tuple-element.198, f32[4,1184]{1,0:T(4,128)S(1)} %get-tuple-element.204, f32[4,1184]{1,0:T(4,128)S(1)} %copy-done.28), kind=kLoop, calls=%fused_computation.4 | loop fusion | flops 22429696 | bytes 56112128 | tf_op jit(solution)/shard_map/while/body/eval_jaxpr/convert_element_type | solution.py:95
  1064.4 8.4 fusion.173
  1073.6 15.1 multiply_convert_fusion.1
  1088.7 7.6 fusion.174
  1101.2 8.6 fusion.43
  1116.4 6.7 pad_maximum_fusion.1
  1139.3 5.6 fusion.101
  1148.1 9.4 fusion.42
  1166.8 6.7 pad_maximum_fusion
  1173.5 8.4 all-to-all-done.3
  1181.9 4.5 all-to-all-start.2
  1186.5 5.7 fusion.96
  1194.5 70.1 %all-reduce = f32[4096]{0:T(1024)S(1)} all-reduce(f32[4096]{0:T(1024)S(1)} %add_dynamic-update-slice_fusion), channel_id=14, replica_groups=mesh['wide'=8,'narrow'=4] {'wide','narrow'}, use_global_device_ids=true, to_apply=%region_36.37.clone | all-reduce | flops 4096 | bytes 32768
  1270.2 69.2 %reduce-scatter.53.cloned.1.call-done = f32[32,2]{1,0:T(8,128)} async-done(((f32[1024,2]{1,0:T(8,128)}), f32[32,2]{1,0:T(8,128)}) %reduce-scatter.53.cloned.1.call-update) | async-done | bytes 272
  1340.7 136.1 %reduce-scatter.51.cloned.1.call-done = f32[32,6]{1,0:T(8,128)} async-done(((f32[1024,6]{1,0:T(8,128)}), f32[32,6]{1,0:T(8,128)}) %reduce-scatter.51.cloned.1.call-update) | async-done | bytes 784
  1478.1 32.0 %reduce-scatter.45.cloned.1.call-done = bf16[128,256]{1,0:T(8,128)(2,1)} async-done(((bf16[1024,256]{1,0:T(8,128)(2,1)}), bf16[128,256]{1,0:T(8,128)(2,1)}) %reduce-scatter.45.cloned.1.call-update) | async-done | bytes 65552
  1511.0 36.3 %reduce-scatter.43.cloned.1.call-done = bf16[128,256]{1,0:T(8,128)(2,1)} async-done(((bf16[1024,256]{1,0:T(8,128)(2,1)}), bf16[128,256]{1,0:T(8,128)(2,1)}) %reduce-scatter.43.cloned.1.call-update) | async-done | bytes 65552
  1549.0 39.9 %reduce-scatter.37.cloned.1.call-done = bf16[128,3,256]{2,0,1:T(8,128)(2,1)} async-done(((bf16[1024,3,256]{2,0,1:T(8,128)(2,1)}), bf16[128,3,256]{2,0,1:T(8,128)(2,1)}) %reduce-scatter.37.cloned.1.call-update) | async-done | bytes 196624 | tf_op jit(solution)/shard_map/reduce_scatter | solution.py:40
  1588.9 42.1 %reduce-scatter.35.cloned.1.call-done = bf16[128,3,256]{2,0,1:T(8,128)(2,1)} async-done(((bf16[1024,3,256]{2,0,1:T(8,128)(2,1)}), bf16[128,3,256]{2,0,1:T(8,128)(2,1)}) %reduce-scatter.35.cloned.1.call-update) | async-done | bytes 196624 | tf_op jit(solution)/shard_map/reduce_scatter | solution.py:40
  1641.5 5.6 fusion.119
  1647.1 4.9 fusion.118
  (324 shorter events, 151.1 us)
Async XLA Ops:
  7.2 31.0 %all-gather.17.cloned.1.call-start = ((), (), s32[]{:S(2)}) async-start(), calls=%async_computation.18 | async-start | bytes 1769472 | tf_op jit(solution)/shard_map/all_gather | solution.py:26
  7.9 124.2 %all-gather.31.cloned.1.call-start = ((), (), s32[]{:S(2)}) async-start(), calls=%async_computation.26 | async-start | bytes 3031040 | tf_op jit(solution)/shard_map/all_gather | solution.py:15
  10.1 28.8 %copy-start.33 = (bf16[256,128]{1,0:T(8,128)(2,1)S(1)}, bf16[256,128]{1,0:T(8,128)(2,1)}, u32[]{:S(2)}) copy-start(bf16[256,128]{1,0:T(8,128)(2,1)} %param.15) | copy-start | bytes 196612
  12.8 37.7 %copy-start.40 = (bf16[6,32]{1,0:T(8,128)(2,1)S(1)}, bf16[6,32]{1,0:T(8,128)(2,1)}, u32[]{:S(2)}) copy-start(bf16[6,32]{1,0:T(8,128)(2,1)} %param.19) | copy-start | bytes 1156
  12.8 194.4 %all-gather.19.cloned.1.call-start = ((), (), s32[]{:S(2)}) async-start(), calls=%async_computation.19 | async-start | bytes 7864320 | tf_op jit(solution)/shard_map/all_gather | solution.py:32
  38.2 220.4 %all-gather.21.cloned.1.call-start = ((), (), s32[]{:S(2)}) async-start(), calls=%async_computation.20 | async-start | bytes 3031040 | tf_op jit(solution)/shard_map/all_gather | solution.py:15
  38.8 416.2 %all-gather.23.cloned.1.call-start = ((), (), s32[]{:S(2)}) async-start(), calls=%async_computation.21 | async-start | bytes 2621440 | tf_op jit(solution)/shard_map/all_gather | solution.py:33
  49.8 477.3 %all-gather.27.cloned.1.call-start = ((), (), s32[]{:S(2)}) async-start(), calls=%async_computation.23 | async-start | bytes 2359296 | tf_op jit(solution)/shard_map/all_gather | solution.py:28
  128.7 200.0 %copy-start.34 = (f32[4,64]{1,0:T(4,128)}, f32[4,64]{1,0:T(4,128)S(1)}, u32[]{:S(2)}) copy-start(f32[4,64]{1,0:T(4,128)S(1)} %add.404) | copy-start | bytes 3076
  128.9 221.9 %copy-start.31 = (f32[4,64]{1,0:T(4,128)}, f32[4,64]{1,0:T(4,128)S(1)}, u32[]{:S(2)}) copy-start(f32[4,64]{1,0:T(4,128)S(1)} %add.401) | copy-start | bytes 3076
  268.1 82.6 %copy-start.2 = (f32[1,1,1184,256]{2,3,1,0:T(8,128)}, f32[1,1,1184,256]{2,3,1,0:T(8,128)S(1)}, u32[]{:S(2)}) copy-start(f32[1,1,1184,256]{2,3,1,0:T(8,128)S(1)} %copy.130) | copy-start | bytes 3637252
  272.9 26.1 %copy-start = (f32[1,1,1184,256]{2,3,1,0:T(8,128)}, f32[1,1,1184,256]{2,3,1,0:T(8,128)S(1)}, u32[]{:S(2)}) copy-start(f32[1,1,1184,256]{2,3,1,0:T(8,128)S(1)} %copy.122) | copy-start | bytes 3637252
  299.0 11.8 copy-start.25
  310.8 13.6 copy-start.15
  313.0 15.8 copy-start.9
  324.4 47.9 %all-to-all-start = ((bf16[4,2,37888]{2,1,0:T(2,128)(2,1)}), bf16[4,2,37888]{2,1,0:T(2,128)(2,1)}, u32[]{:S(2)}, u32[]{:S(2)}) async-start(bf16[4,2,37888]{2,1,0:T(2,128)(2,1)} %reshape.1164), calls=%async_computation | async-start | bytes 1212416 | tf_op jit(solution)/shard_map/all_to_all | solution.py:169
  350.7 11.8 copy-start.27
  362.5 9.8 copy-start.16
  364.9 12.4 copy-start.41
  372.3 80.9 %all-to-all-start.1 = ((bf16[4,2,37888]{2,1,0:T(2,128)(2,1)}), bf16[4,2,37888]{2,1,0:T(2,128)(2,1)S(1)}, u32[]{:S(2)}, u32[]{:S(2)}) async-start(bf16[4,2,37888]{2,1,0:T(2,128)(2,1)} %reshape.1162), calls=%async_computation.2 | async-start | bytes 1212416 | tf_op jit(solution)/shard_map/all_to_all | solution.py:169
  377.3 149.9 %all-gather.33.cloned.1.call-start = ((), (), s32[]{:S(2)}) async-start(), calls=%async_computation.27 | async-start | bytes 3031040 | tf_op jit(solution)/shard_map/all_gather | solution.py:15
  460.9 83.0 %all-gather.29.cloned.1.call-start = ((), (), s32[]{:S(2)}) async-start(), calls=%async_computation.24 | async-start | bytes 2359296 | tf_op jit(solution)/shard_map/all_gather | solution.py:29
  461.7 130.2 %all-gather.25.cloned.1.call-start = ((), (), s32[]{:S(2)}) async-start(), calls=%async_computation.22 | async-start | bytes 3031040 | tf_op jit(solution)/shard_map/all_gather | solution.py:15
  527.1 114.7 %reduce-scatter.29.cloned.1.call-start = ((), (), s32[]{:S(2)}) async-start(), calls=%async_computation.28 | async-start | bytes 3031040 | tf_op jit(solution)/shard_map/reduce_scatter | solution.py:19
  550.4 142.7 %reduce-scatter.27.cloned.1.call-start = ((), (), s32[]{:S(2)}) async-start(), calls=%async_computation.25 | async-start | bytes 3031040 | tf_op jit(solution)/shard_map/reduce_scatter | solution.py:19
  591.9 18.5 %copy-start.47 = (bf16[1024,1024]{1,0:T(8,128)(2,1)S(1)}, bf16[1024,1024]{1,0:T(8,128)(2,1)}, u32[]{:S(2)}) copy-start(bf16[1024,1024]{1,0:T(8,128)(2,1)} %all-gather.29.cloned.1.call-done) | copy-start | bytes 6291460
  614.3 78.8 %copy-start.37 = (f32[1,1024]{1,0:T(1,128)S(1)}, f32[1,1024]{1,0:T(1,128)}, u32[]{:S(2)}) copy-start(f32[1,1024]{1,0:T(1,128)} %get-tuple-element.173) | copy-start | bytes 12292
  614.3 137.1 %all-gather.35.cloned.1.call-start = ((), (), s32[]{:S(2)}) async-start(), calls=%async_computation.29 | async-start | bytes 3031040 | tf_op jit(solution)/shard_map/all_gather | solution.py:15
  700.6 102.3 %all-gather.39.cloned.1.call-start = ((), (), s32[]{:S(2)}) async-start(), calls=%async_computation.32 | async-start | bytes 3031040 | tf_op jit(solution)/shard_map/all_gather | solution.py:15
  701.4 152.0 %reduce-scatter.31.cloned.1.call-start = ((), (), s32[]{:S(2)}) async-start(), calls=%async_computation.30 | async-start | bytes 3031040 | tf_op jit(solution)/shard_map/reduce_scatter | solution.py:19
  751.4 11.5 copy-start.45
  766.9 137.1 %reduce-scatter.33.cloned.1.call-start = ((), (), s32[]{:S(2)}) async-start(), calls=%async_computation.33 | async-start | bytes 3031040 | tf_op jit(solution)/shard_map/reduce_scatter | solution.py:19
  802.9 11.5 copy-start.46
  818.5 142.7 %all-gather.41.cloned.1.call-start = ((), (), s32[]{:S(2)}) async-start(), calls=%async_computation.34 | async-start | bytes 3031040 | tf_op jit(solution)/shard_map/all_gather | solution.py:15
  853.3 50.7 %copy-start.22 = (bf16[1,296,1024]{2,1,0:T(8,128)(2,1)S(1)}, bf16[1,296,1024]{2,1,0:T(8,128)(2,1)}, u32[]{:S(2)}) copy-start(bf16[1,296,1024]{2,1,0:T(8,128)(2,1)} %reduce-scatter.31.cloned.1.call-done) | copy-start | bytes 1818628
  910.4 102.7 %all-gather.37.cloned.1.call-start = ((), (), s32[]{:S(2)}) async-start(), calls=%async_computation.31 | async-start | bytes 3031040 | tf_op jit(solution)/shard_map/all_gather | solution.py:15
  911.4 353.7 %reduce-scatter.49.cloned.1.call-start = ((), (), s32[]{:S(2)}) async-start(), calls=%async_computation.42 | async-start | bytes 2359296
  919.4 346.8 %reduce-scatter.47.cloned.1.call-start = ((), (), s32[]{:S(2)}) async-start(), calls=%async_computation.41 | async-start | bytes 2359296
  927.5 340.8 %reduce-scatter.41.cloned.1.call-start = ((), (), s32[]{:S(2)}) async-start(), calls=%async_computation.38 | async-start | bytes 2359296 | tf_op jit(solution)/shard_map/reduce_scatter | solution.py:46
  934.4 333.9 %reduce-scatter.39.cloned.1.call-start = ((), (), s32[]{:S(2)}) async-start(), calls=%async_computation.37 | async-start | bytes 2359296 | tf_op jit(solution)/shard_map/reduce_scatter | solution.py:46
  940.2 399.1 %reduce-scatter.53.cloned.1.call-start = ((), (), s32[]{:S(2)}) async-start(), calls=%async_computation.44 | async-start | bytes 540672
  941.5 22.6 %copy-start.28 = (f32[4,1184]{1,0:T(4,128)S(1)}, f32[4,1184]{1,0:T(4,128)}, u32[]{:S(2)}) copy-start(f32[4,1184]{1,0:T(4,128)} %copy-done.27) | copy-start | bytes 56836
  941.5 535.3 %reduce-scatter.51.cloned.1.call-start = ((), (), s32[]{:S(2)}) async-start(), calls=%async_computation.43 | async-start | bytes 540672
  964.1 11.8 copy-start.3
  964.1 11.8 copy-start.32
  991.0 24.9 %copy-start.26 = (f32[4,1184]{1,0:T(4,128)S(1)}, f32[4,1184]{1,0:T(4,128)}, u32[]{:S(2)}) copy-start(f32[4,1184]{1,0:T(4,128)} %copy-done.25) | copy-start | bytes 56836
  1016.0 10.8 copy-start.1
  1042.0 22.4 %copy-start.20 = (bf16[1,1,1184,256]{2,3,1,0:T(8,128)(2,1)S(1)}, bf16[1,1,1184,256]{2,3,1,0:T(8,128)(2,1)}, u32[]{:S(2)}) copy-start(bf16[1,1,1184,256]{2,3,1,0:T(8,128)(2,1)} %copy.132) | copy-start | bytes 1818628
  1042.0 30.8 %slice-start = ((s8[24248320]{0:T(1024)(128)(4,1)}), s8[4194304]{0:T(1024)(128)(4,1)S(1)}, s32[]{:S(2)}) async-start(s8[24248320]{0:T(1024)(128)(4,1)} %bitcast.256), calls=%async_computation.45 | async-start | bytes 8388608
  1042.0 30.8 %slice-start.1 = ((s8[24248320]{0:T(1024)(128)(4,1)}), s8[4194304]{0:T(1024)(128)(4,1)S(1)}, s32[]{:S(2)}) async-start(s8[24248320]{0:T(1024)(128)(4,1)} %bitcast.256), calls=%async_computation.46 | async-start | bytes 8388608
  1042.0 30.8 %slice-start.2 = ((s8[24248320]{0:T(1024)(128)(4,1)}), s8[4194304]{0:T(1024)(128)(4,1)S(1)}, s32[]{:S(2)}) async-start(s8[24248320]{0:T(1024)(128)(4,1)} %bitcast.256), calls=%async_computation.47 | async-start | bytes 8388608
  1042.0 30.8 %slice-start.3 = ((s8[24248320]{0:T(1024)(128)(4,1)}), s8[4194304]{0:T(1024)(128)(4,1)S(1)}, s32[]{:S(2)}) async-start(s8[24248320]{0:T(1024)(128)(4,1)} %bitcast.256), calls=%async_computation.48 | async-start | bytes 8388608
  1042.0 30.8 %slice-start.4 = ((s8[24248320]{0:T(1024)(128)(4,1)}), s8[4194304]{0:T(1024)(128)(4,1)S(1)}, s32[]{:S(2)}) async-start(s8[24248320]{0:T(1024)(128)(4,1)} %bitcast.256), calls=%async_computation.49 | async-start | bytes 8388608
  1064.4 9.2 slice-start.5
  1072.8 41.4 %copy-start.7 = (bf16[1184,4,64]{0,2,1:T(8,128)(2,1)}, bf16[1184,4,64]{0,2,1:T(8,128)(2,1)S(1)}, u32[]{:S(2)}) copy-start(bf16[1184,4,64]{0,2,1:T(8,128)(2,1)S(1)} %get-tuple-element.162) | copy-start | bytes 1818628
  1073.6 15.1 copy-start.19
  1088.7 8.9 copy-start.17
  1097.5 412.6 %reduce-scatter.45.cloned.1.call-start = ((), (), s32[]{:S(2)}) async-start(), calls=%async_computation.40 | async-start | bytes 589824
  1123.1 58.9 %all-to-all-start.3 = ((bf16[3,1,1184,256]{3,0,1,2:T(4,128)(2,1)}), bf16[3,1,1184,256]{3,0,1,2:T(4,128)(2,1)S(1)}, u32[]{:S(2)}, u32[]{:S(2)}) async-start(bf16[3,1,1184,256]{3,0,1,2:T(4,128)(2,1)} %pad_maximum_fusion.1), calls=%async_computation.7 | async-start | bytes 4849664 | tf_op jit(solution)/shard_map/all_to_all | solution.py:236
  1126.7 420.6 %reduce-scatter.43.cloned.1.call-start = ((), (), s32[]{:S(2)}) async-start(), calls=%async_computation.39 | async-start | bytes 589824
  1132.4 456.4 %reduce-scatter.37.cloned.1.call-start = ((), (), s32[]{:S(2)}) async-start(), calls=%async_computation.36 | async-start | bytes 1769472 | tf_op jit(solution)/shard_map/reduce_scatter | solution.py:40
  1148.1 11.7 copy-start.6
  1181.9 454.3 %all-to-all-start.2 = ((bf16[3,1,1184,256]{3,0,1,2:T(4,128)(2,1)}), bf16[3,1,1184,256]{3,0,1,2:T(4,128)(2,1)}, u32[]{:S(2)}, u32[]{:S(2)}) async-start(bf16[3,1,1184,256]{3,0,1,2:T(4,128)(2,1)} %pad_maximum_fusion), calls=%async_computation.5 | async-start | bytes 4849664 | tf_op jit(solution)/shard_map/all_to_all | solution.py:236
  1186.4 444.5 %reduce-scatter.35.cloned.1.call-start = ((), (), s32[]{:S(2)}) async-start(), calls=%async_computation.35 | async-start | bytes 1769472 | tf_op jit(solution)/shard_map/reduce_scatter | solution.py:40
  (24 other events, 85.8 us)
Sparse Core Ops, SparseCore 0:
  9.9 28.2 all-gather.16
  39.8 52.0 all-gather.30
  93.4 113.7 all-gather.18
  209.2 49.4 all-gather.20
  260.0 44.2 all-gather.22
  306.1 26.5 all-gather.26
  461.0 48.7 all-gather.32
  511.7 26.7 all-gather.28
  540.6 51.2 all-gather.24
  594.0 47.6 reduce-scatter.28
  644.6 48.4 reduce-scatter.26
  700.7 50.6 all-gather.34
  753.0 49.8 all-gather.38
  805.6 47.6 reduce-scatter.30
  855.5 48.4 reduce-scatter.32
  910.5 50.6 all-gather.40
  963.2 49.8 all-gather.36
  1016.2 39.7 reduce-scatter.48
  1059.3 41.0 reduce-scatter.46
  1103.6 41.1 reduce-scatter.40
  1148.0 41.1 reduce-scatter.38
  1191.4 147.8 reduce-scatter.52
  1341.6 135.1 reduce-scatter.50
  1479.7 30.3 reduce-scatter.44
  1513.2 34.1 reduce-scatter.42
  1550.5 38.3 reduce-scatter.36
  1592.6 38.3 reduce-scatter.34
where the time goes:
time: 1670 us; the launch traced here: 1660 us
  waiting for transfers between devices  844 us (51%)
  blocking collectives  297 us (18%)
  matrix products  275 us (16%)
  other arithmetic  120 us (7%)
  local copies, waits for them, and re-layouts  89.7 us (5%)
  starting transfers between devices  19.5 us (1%)
    unnamed x33, waiting for transfers between devices  277 us
    all_gather x8, waiting for transfers between devices, spread_rows(): return lax.all_gather(piece, 'narrow', axis=1, tiled=True)  215 us
    reduce_scatter x4, waiting for transfers between devices, collect_sums(): lax.psum_scatter(term.astype(jnp.bfloat16), 'narrow', scatter_dimension=1...  162 us
    reduce_scatter x2, waiting for transfers between devices, reduce_grads(): lax.psum_scatter(grad_set[0].astype(jnp.bfloat16), 'wide', scatter_dimens...  82 us
    all_gather x1, blocking collectives, shards(): lax.all_gather(biases, ('wide', 'narrow'), axis=1, tiled=True)  77.5 us
    all_gather x1, waiting for transfers between devices, fetch_weights(): lax.all_gather(full_qkv, 'narrow', axis=2, tiled=True)  75 us
    all_gather x1, blocking collectives, shards(): lax.all_gather(gains, ('wide', 'narrow'), axis=1, tiled=True)  72.9 us
    unnamed x1, blocking collectives  70.1 us
  transfers between devices with their start and end apart: 31, of which 19 were waited for; matrix products, arithmetic and copies ran while one was open for 27% of the time, Pallas kernels for 0%

commit v1 on v0

--- a/solution.py
+++ b/solution.py
@@ -9,6 +9,8 @@
 ITEM = 592
 NOISE = 25
 MB = 2
+KEYS = 512
+PAIRS = ((0, 1), (1, 0), (2, 3), (3, 2))
 
 
 def spread_rows(piece):
@@ -280,6 +282,152 @@
     )
 
 
+def trade_halves(piece, even):
+    own = jnp.where(even, piece[0], piece[1])
+    give = jnp.where(even, piece[1], piece[0])
+    got = lax.ppermute(give, "narrow", PAIRS)
+    first = jnp.where(even, own, got)
+    second = jnp.where(even, got, own)
+    return jnp.concatenate([first, second], 0)
+
+
+def return_halves(item, even):
+    half = item.shape[0] // 2
+    own = jnp.where(even, item[:half], item[half:])
+    give = jnp.where(even, item[half:], item[:half])
+    got = lax.ppermute(give, "narrow", PAIRS)
+    return jnp.stack([jnp.where(even, own, got), jnp.where(even, got, own)])
+
+
+def gather_all(shard):
+    return lax.all_gather(shard, ("wide", "narrow"), axis=0, tiled=False)
+
+
+def scatter_all(blocks):
+    return lax.psum_scatter(
+        blocks.astype(jnp.bfloat16), ("wide", "narrow"), scatter_dimension=0, tiled=False
+    ).astype(jnp.float32)
+
+
+def mm(spec, left, right):
+    return jnp.einsum(spec, left, right, preferred_element_type=jnp.float32)
+
+
+def item_shards(
+    tokens, timestep, context, w_qkv, w_out, w_up, w_down, b_up, biases, gains, cotangent
+):
+    wide = lax.axis_size("wide")
+    narrow = lax.axis_size("narrow")
+    z = lax.axis_index("narrow")
+    even = z % 2 == 0
+    width = tokens.shape[2]
+    heads = width // HEAD_DIM
+    bias_all, gain_all, up_bias = (
+        lax.all_gather(biases, ("wide", "narrow"), axis=1, tiled=True).astype(jnp.float32),
+        lax.all_gather(gains, ("wide", "narrow"), axis=1, tiled=True).astype(jnp.float32),
+        lax.all_gather(b_up, ("wide", "narrow"), axis=0, tiled=True).astype(jnp.float32),
+    )
+    token_item = trade_halves(tokens, even).astype(jnp.float32)
+    cot = trade_halves(cotangent, even).astype(jnp.float32)
+    row = z % 2
+    embed = jnp.where(even, timestep[0], timestep[1]).astype(jnp.float32)
+    start = context[row, z // 2]
+    offset = jnp.arange(ITEM, dtype=jnp.int32)
+    noisy = (offset >= start) & (offset < start + NOISE)
+    valid = offset[:KEYS] < start + NOISE
+    x = token_item + jnp.where(noisy[:, None], embed[None], 0.0)
+    xr = x.astype(jnp.bfloat16)
+
+    all_qkv = gather_all(w_qkv.transpose(1, 0, 2))
+    all_out = gather_all(w_out)
+    all_up = gather_all(w_up)
+    all_down = gather_all(w_down)
+    wq = all_qkv.reshape(wide, narrow, 3, -1, w_qkv.shape[2])
+    wq = wq.transpose(2, 0, 3, 1, 4).reshape(3, width, width)
+    wo = all_out.reshape((wide, narrow) + w_out.shape).transpose(1, 2, 0, 3).reshape(width, width)
+    wu = all_up.reshape((wide, narrow) + w_up.shape).transpose(0, 2, 1, 3).reshape(width, -1)
+    wd = all_down.reshape((wide, narrow) + w_down.shape).transpose(1, 2, 0, 3).reshape(-1, width)
+
+    q = (mm("sd,df->sf", xr, wq[0]) + bias_all[0]).astype(jnp.bfloat16)
+    k = mm("sd,df->sf", xr[:KEYS], wq[1]).astype(jnp.bfloat16)
+    v = (mm("sd,df->sf", xr[:KEYS], wq[2]) + bias_all[1]).astype(jnp.bfloat16)
+    q = q.reshape(ITEM, heads, HEAD_DIM)
+    k = k.reshape(KEYS, heads, HEAD_DIM)
+    v = v.reshape(KEYS, heads, HEAD_DIM)
+    scale = HEAD_DIM**-0.5
+    scores = jnp.where(valid, mm("qhe,khe->hqk", q, k) * scale, -jnp.inf)
+    probs = jax.nn.softmax(scores, axis=-1)
+    low = probs.astype(jnp.bfloat16)
+    attended = mm("hqk,khe->qhe", low, v).reshape(ITEM, width).astype(jnp.bfloat16)
+    h1 = x + mm("sf,fd->sd", attended, wo) + bias_all[2]
+    y1, n1, s1 = norm_forward(h1, gain_all[0], bias_all[4])
+    y1r = y1.astype(jnp.bfloat16)
+    pre = mm("sd,df->sf", y1r, wu) + up_bias
+    act, pull = jax.vjp(partial(jax.nn.gelu, approximate=False), pre)
+    act = act.astype(jnp.bfloat16)
+    h2 = y1 + mm("sf,fd->sd", act, wd) + bias_all[3]
+    result, n2, s2 = norm_forward(h2, gain_all[1], bias_all[5])
+    output = return_halves(result.astype(jnp.bfloat16), even)
+
+    dh2 = norm_backward(cot, n2, s2, gain_all[1])
+    dh2r = dh2.astype(jnp.bfloat16)
+    d_pre = pull(mm("sd,fd->sf", dh2r, wd))[0]
+    d_prer = d_pre.astype(jnp.bfloat16)
+    g_down = mm("sf,sd->fd", act, dh2r)
+    g_down = g_down.reshape((narrow, w_down.shape[0], wide, -1)).transpose(2, 0, 1, 3)
+    g_down = scatter_all(g_down.reshape((wide * narrow,) + w_down.shape))
+    g_up = mm("sd,sf->df", y1r, d_prer)
+    g_up = g_up.reshape((wide, w_up.shape[0], narrow, -1)).transpose(0, 2, 1, 3)
+    g_up = scatter_all(g_up.reshape((wide * narrow,) + w_up.shape))
+    dy1 = dh2 + mm("sf,df->sd", d_prer, wu)
+    dh1 = norm_backward(dy1, n1, s1, gain_all[0])
+    dh1r = dh1.astype(jnp.bfloat16)
+    g_out = mm("sf,sd->fd", attended, dh1r)
+    g_out = g_out.reshape((narrow, w_out.shape[0], wide, -1)).transpose(2, 0, 1, 3)
+    g_out = scatter_all(g_out.reshape((wide * narrow,) + w_out.shape))
+    d_att = mm("sd,fd->sf", dh1r, wo).astype(jnp.bfloat16).reshape(ITEM, heads, HEAD_DIM)
+    d_prob = mm("qhe,khe->hqk", d_att, v)
+    d_score = probs * (d_prob - jnp.sum(probs * d_prob, -1, keepdims=True))
+    d_score = d_score.astype(jnp.bfloat16)
+    d_q = (mm("hqk,khe->qhe", d_score, k) * scale).reshape(ITEM, width)
+    d_k = (mm("hqk,qhe->khe", d_score, q) * scale).reshape(KEYS, width)
+    d_v = mm("hqk,qhe->khe", low, d_att).reshape(KEYS, width)
+    dq, dk, dv = (d_q.astype(jnp.bfloat16), d_k.astype(jnp.bfloat16), d_v.astype(jnp.bfloat16))
+    g_qkv = jnp.stack(
+        [
+            mm("sd,sf->df", xr, dq),
+            mm("sd,sf->df", xr[:KEYS], dk),
+            mm("sd,sf->df", xr[:KEYS], dv),
+        ]
+    )
+    g_qkv = g_qkv.reshape(3, wide, -1, narrow, w_qkv.shape[2]).transpose(1, 3, 0, 2, 4)
+    g_qkv = scatter_all(g_qkv.reshape((wide * narrow, 3) + g_qkv.shape[3:])).transpose(1, 0, 2)
+    d_x = dh1 + mm("sf,df->sd", dq, wq[0])
+    d_keys_x = mm("sf,df->sd", dk, wq[1]) + mm("sf,df->sd", dv, wq[2])
+    d_x = d_x + jnp.pad(d_keys_x, ((0, ITEM - KEYS), (0, 0)))
+    grad_tokens = return_halves(d_x.astype(jnp.bfloat16), even).astype(jnp.float32)
+
+    bias_terms = jnp.stack(
+        [
+            jnp.sum(d_q, 0),
+            jnp.sum(d_v, 0),
+            jnp.sum(dh1, 0),
+            jnp.sum(dh2, 0),
+            jnp.sum(dy1, 0),
+            jnp.sum(cot, 0),
+        ]
+    )
+    gain_terms = jnp.stack([jnp.sum(dy1 * n1, 0), jnp.sum(cot * n2, 0)])
+    grad_b_up, grad_biases, grad_gains = (
+        lax.psum_scatter(
+            jnp.sum(d_pre, 0), ("wide", "narrow"), scatter_dimension=0, tiled=True
+        ),
+        lax.psum_scatter(bias_terms, ("wide", "narrow"), scatter_dimension=1, tiled=True),
+        lax.psum_scatter(gain_terms, ("wide", "narrow"), scatter_dimension=1, tiled=True),
+    )
+    return (output, grad_tokens, g_qkv, g_out, g_up, g_down, grad_b_up, grad_biases, grad_gains)
+
+
 def solution(mesh):
     placed = (
         P("wide", "narrow", None),
@@ -294,8 +442,9 @@
         P(None, ("wide", "narrow")),
         P("wide", "narrow", None),
     )
+    by_item = mesh.shape["narrow"] == 4 and mesh.shape["wide"] == 8
     return jax.shard_map(
-        shards,
+        item_shards if by_item else shards,
         mesh=mesh,
         in_specs=placed,
         out_specs=(

time: 1670 us -> 1360 us (0.81)
  waiting for transfers between devices: 844 us -> 734 us
  matrix products: 275 us -> 170 us
  other arithmetic: 120 us -> 40.6 us
  local copies, waits for them, and re-layouts: 89.7 us -> 130 us
  blocking collectives: 297 us -> 257 us
    reduce_scatter x8 -> x4, waiting for transfers between devices: 244 us -> 620 us  [scatter_all(): lax.psum_scatter(blocks.astype(jnp.bfloat16), ('wide', 'narrow'), scatter...]
    all_gather x13 -> x4, waiting for transfers between devices: 315 us -> 0.03 us  [gather_all(): return lax.all_gather(shard, ('wide', 'narrow'), axis=0, tiled=False)]
    unnamed x33 -> x12, waiting for transfers between devices: 277 us -> 115 us
    dot_general x36 -> x23, matrix products: 275 us -> 159 us  [mm(): return jnp.einsum(spec, left, right, preferred_element_type=jnp.float32)]
    convert_element_type x6 -> x14, local copies, waits for them, and re-layouts: 5.2 us -> 53.1 us  [the longest x6 44.6 us: scatter_all(): blocks.astype(jnp.bfloat16)]
    reshape x0 -> x4, local copies, waits for them, and re-layouts: none -> 38.3 us  [the longest x1 12.8 us: item_shards(): all_up.reshape((wide, narrow) + w_up.shape).transpose(0, 2, 1, 3)]
    unnamed x1, blocking collectives: 70.1 us -> 37.7 us
    another operation x15 -> x4, local copies, waits for them, and re-layouts: 30.6 us -> 1.99 us  [the longest x12 25.5 us: shards(): d_proj = jnp.stack([d_queries, d_keys, d_values]).astype(jnp.bfloat16)]
  transfers between devices with their start and end apart: 31 -> 14, of which waited for: 19 -> 5; matrix products, arithmetic and copies ran while one was open for 27% -> 15% of each run, Pallas kernels for 0% -> 0%
where the time goes in v1:
time: 1360 us; the launch traced here: 1350 us
  waiting for transfers between devices  734 us (54%)
  blocking collectives  257 us (19%)
  matrix products  170 us (12%)
  local copies, waits for them, and re-layouts  130 us (10%)
  other arithmetic  40.6 us (3%)
  between operations  15.7 us (1%)
    reduce_scatter x4, waiting for transfers between devices, scatter_all(): lax.psum_scatter(blocks.astype(jnp.bfloat16), ('wide', 'narrow'), scatter...  620 us
    dot_general x23, matrix products, mm(): return jnp.einsum(spec, left, right, preferred_element_type=jnp.float32)  159 us
    unnamed x12, waiting for transfers between devices  115 us
    all_gather x1, blocking collectives, item_shards(): lax.all_gather(gains, ('wide', 'narrow'), axis=1, tiled=True)  88.4 us
    all_gather x1, blocking collectives, item_shards(): lax.all_gather(b_up, ('wide', 'narrow'), axis=0, tiled=True)  66.7 us
    all_gather x1, blocking collectives, item_shards(): lax.all_gather(biases, ('wide', 'narrow'), axis=1, tiled=True)  64.5 us
    convert_element_type x6, local copies, waits for them, and re-layouts, scatter_all(): blocks.astype(jnp.bfloat16)  44.6 us
    unnamed x1, blocking collectives  37.7 us
  transfers between devices with their start and end apart: 14, of which 5 were waited for; matrix products, arithmetic and copies ran while one was open for 15% of the time, Pallas kernels for 0%

profile of v1, /device:TPU:0, one launch (start us, length us, event | category | flops | bytes accessed | tf_op | source)
XLA Modules:
  0.0 1354.1 jit_solution(7673460192819993504)
XLA Ops:
  11.4 3.1 collective-permute-start
  16.7 88.4 %all-gather.5 = bf16[32,32,2]{1,2,0:T(2,128)(2,1)S(1)} all-gather(bf16[1,32,2]{1,2,0:T(2,128)(2,1)S(1)} %bitcast.348), channel_id=1, replica_groups=mesh['wide'=8,'narrow'=4] {'wide','narrow'}, dimensions={0}, use_global_device_ids=true | all-gather | bytes 4224 | tf_op jit(solution)/shard_map/all_gather | solution.py:327
  105.1 64.5 %all-gather.4 = bf16[32,32,6]{1,2,0:T(8,128)(2,1)S(1)} all-gather(bf16[1,32,6]{1,2,0:T(8,128)(2,1)S(1)} %bitcast.347), channel_id=1, replica_groups=mesh['wide'=8,'narrow'=4] {'wide','narrow'}, dimensions={0}, use_global_device_ids=true | all-gather | bytes 12672 | tf_op jit(solution)/shard_map/all_gather | solution.py:326
  169.9 66.7 %all-gather.6 = bf16[32,1,128]{2,1,0:T(2,128)(2,1)S(1)} all-gather(bf16[1,1,128]{2,1,0:T(2,128)(2,1)S(1)} %bitcast.349), channel_id=1, replica_groups=mesh['wide'=8,'narrow'=4] {'wide','narrow'}, dimensions={0}, use_global_device_ids=true | all-gather | bytes 8448 | tf_op jit(solution)/shard_map/all_gather | solution.py:328
  240.9 2.7 bitcast_select_fusion.1
  243.6 4.2 copy.84
  247.9 9.1 copy.79
  257.0 5.3 fusion.114
  263.7 2.5 add_convert_fusion.2
  266.1 1.7 copy.82
  267.8 4.8 fusion.80
  272.6 2.3 copy.83
  274.9 3.9 add_convert_fusion.3
  278.8 1.5 copy.81
  280.3 11.3 fusion.117
  291.7 8.7 fusion.64
  301.1 2.0 dot_general.135
  303.1 3.8 fusion.118
  307.3 12.8 copy.86
  320.1 12.1 copy.87
  332.2 30.2 %multiply_convert_fusion.1 = (bf16[592,4096]{1,0:T(8,128)(2,1)S(1)}, f32[592,4096]{1,0:T(8,128)}, f32[592,4096]{1,0:T(8,128)}) fusion(f32[4096]{0:T(1024)S(1)} %bitcast.334, bf16[512,8,8,128]{3,2,1,0:T(8,128)(2,1)} %bitcast.283, f32[592,1024]{1,0:T(8,128)S(1)} %get-tuple-element.46, f32[1024]{0:T(1024)S(1)} %bitcast.339, f32[1024]{0:T(1024)S(1)} %bitcast.327, ...), kind=kOutput, calls=%fused_computation.9 | convolution fusion | flops 5129125888 | bytes 35091072 | tf_op jit(solution)/shard_map/sd,df->sf/dot_general | solution.py:313
  362.5 5.4 fusion.119
  370.2 2.5 fusion.110
  372.7 18.2 %fusion.120 = (f32[4096]{0:T(1024)}, bf16[592,4096]{1,0:T(8,128)(2,1)}) fusion(f32[592,4096]{1,0:T(8,128)} %get-tuple-element.22, bf16[512,8,8,128]{3,2,1,0:T(8,128)(2,1)} %bitcast.285, f32[592,1024]{1,0:T(8,128)S(1)} %get-tuple-element.18, f32[592,4096]{1,0:T(8,128)} %get-tuple-element.47, f32[4096]{0:T(1024)S(1)} %bitcast.335), kind=kOutput, calls=%fused_computation.180 | convolution fusion | flops 5005455360 | bytes 35094528 | tf_op jit(solution)/shard_map/sd,fd->sf/dot_general | solution.py:313
  390.9 10.7 multiply_reduce_fusion.1
  402.3 1.4 copy-done.18
  403.8 1.5 fusion.67
  406.0 13.0 multiply_reduce_fusion
  419.0 9.3 bitcast_convert_fusion.1
  428.3 13.1 multiply_convert_fusion
  441.4 2.9 bitcast_convert_fusion
  446.5 1.8 bitcast_reduce_fusion.1
  449.6 3.5 convert_bitcast_fusion.1
  453.2 1.5 copy.98
  454.9 1.4 copy.125
  456.7 1.8 copy.102
  458.5 1.5 copy.89
  459.9 3.3 convert_bitcast_fusion.4
  464.6 5.7 multiply_convert_fusion.2
  472.2 3.0 copy.94
  475.3 1.6 copy-done.5
  476.9 12.0 convolution_convert_fusion
  489.0 14.6 %convert_element_type.201 = bf16[8,128,4,1024]{3,2,1,0:T(4,128)(2,1)} reshape(bf16[1024,4096]{1,0:T(8,128)(2,1)} %convolution_convert_fusion) | data formatting | bytes 16777216 | tf_op jit(solution)/shard_map/convert_element_type | solution.py:308
  503.6 9.8 copy.99
  513.4 1.6 copy-done.17
  515.1 11.5 convert_bitcast_fusion
  526.6 8.8 copy.127
  535.4 7.2 bitcast_bitcast_fusion
  542.5 8.5 copy.100
  553.3 3.0 fusion.42
  559.1 1.5 add_convert_fusion
  561.5 2.0 collective-permute-start.3
  563.5 37.7 %all-reduce.1 = f32[4096]{0:T(1024)S(1)} all-reduce(f32[4096]{0:T(1024)S(1)} %copy-done.34), channel_id=10, replica_groups=mesh['wide'=8,'narrow'=4] {'wide','narrow'}, use_global_device_ids=true, to_apply=%region_16.17.clone | all-reduce | flops 4096 | bytes 32768
  603.1 112.2 %reduce-scatter.19.cloned.1.call-done = f32[32,6]{1,0:T(8,128)} async-done(((f32[1024,6]{1,0:T(8,128)}), f32[32,6]{1,0:T(8,128)}) %reduce-scatter.19.cloned.1.call-update) | async-done | bytes 784
  715.4 1.4 copy.114
  719.2 1.6 maximum_convert_fusion
  720.8 133.7 %reduce-scatter.13.cloned.1.call-done = bf16[1,256,128]{2,1,0:T(8,128)(2,1)} async-done(((bf16[32,256,128]{2,1,0:T(8,128)(2,1)}), bf16[1,256,128]{2,1,0:T(8,128)(2,1)}) %reduce-scatter.13.cloned.1.call-update) | async-done | bytes 65552 | tf_op jit(solution)/shard_map/reduce_scatter | solution.py:307
  854.5 1.5 bitcast_convert_fusion.4
  856.0 116.8 %reduce-scatter.11.cloned.1.call-done = bf16[1,3,128,256]{3,2,1,0:T(8,128)(2,1)} async-done(((bf16[32,3,128,256]{3,2,1,0:T(8,128)(2,1)}), bf16[1,3,128,256]{3,2,1,0:T(8,128)(2,1)}) %reduce-scatter.11.cloned.1.call-update) | async-done | bytes 196624 | tf_op jit(solution)/shard_map/reduce_scatter | solution.py:307
  972.7 1.7 convert_bitcast_fusion.6
  974.4 185.3 %reduce-scatter.15.cloned.1.call-done = bf16[1,128,1024]{2,1,0:T(8,128)(2,1)} async-done(((bf16[32,128,1024]{2,1,0:T(8,128)(2,1)}), bf16[1,128,1024]{2,1,0:T(8,128)(2,1)}) %reduce-scatter.15.cloned.1.call-update) | async-done | bytes 262160 | tf_op jit(solution)/shard_map/reduce_scatter | solution.py:307
  1159.7 1.8 bitcast_convert_fusion.3
  1161.5 183.8 %reduce-scatter.17.cloned.1.call-done = bf16[1,1024,128]{2,1,0:T(8,128)(2,1)} async-done(((bf16[32,1024,128]{2,1,0:T(8,128)(2,1)}), bf16[1,1024,128]{2,1,0:T(8,128)(2,1)}) %reduce-scatter.17.cloned.1.call-update) | async-done | bytes 262160 | tf_op jit(solution)/shard_map/reduce_scatter | solution.py:307
  1345.3 1.8 bitcast_convert_fusion.2
  (165 shorter events, 34.0 us)
Async XLA Ops:
  7.2 7.4 copy-start.14
  7.2 8.3 copy-start.40
  7.2 9.5 copy-start.38
  7.2 97.9 %copy-start.37 = (bf16[6,32]{1,0:T(8,128)(2,1)S(1)}, bf16[6,32]{1,0:T(8,128)(2,1)}, u32[]{:S(2)}) copy-start(bf16[6,32]{1,0:T(8,128)(2,1)} %param.19) | copy-start | bytes 1156
  7.2 162.4 %copy-start.35 = (bf16[2,1024]{1,0:T(2,128)(2,1)S(1)}, bf16[2,1024]{1,0:T(2,128)(2,1)}, u32[]{:S(2)}) copy-start(bf16[2,1024]{1,0:T(2,128)(2,1)} %param.12) | copy-start | bytes 12292
  7.2 236.4 %all-gather.14.cloned.1.call-start = ((), (), s32[]{:S(2)}) async-start(), calls=%async_computation.11 | async-start | bytes 2162688 | tf_op jit(solution)/shard_map/all_gather | solution.py:303
  8.0 239.9 %all-gather.12.cloned.1.call-start = ((), (), s32[]{:S(2)}) async-start(), calls=%async_computation.10 | async-start | bytes 6488064 | tf_op jit(solution)/shard_map/all_gather | solution.py:303
  8.0 161.9 %copy-start.39 = (bf16[128]{0:T(256)(128)(2,1)S(1)}, bf16[128]{0:T(256)(128)(2,1)}, u32[]{:S(2)}) copy-start(bf16[128]{0:T(256)(128)(2,1)} %param.18) | copy-start | bytes 772
  8.7 229.8 %copy-start.13 = (bf16[2,296,1024]{2,1,0:T(8,128)(2,1)S(1)}, bf16[2,296,1024]{2,1,0:T(8,128)(2,1)}, u32[]{:S(2)}) copy-start(bf16[2,296,1024]{2,1,0:T(8,128)(2,1)} %param.11) | copy-start | bytes 3637252
  8.7 298.6 %all-gather.16.cloned.1.call-start = ((), (), s32[]{:S(2)}) async-start(), calls=%async_computation.12 | async-start | bytes 8650752 | tf_op jit(solution)/shard_map/all_gather | solution.py:303
  9.5 310.6 %all-gather.18.cloned.1.call-start = ((), (), s32[]{:S(2)}) async-start(), calls=%async_computation.13 | async-start | bytes 8650752 | tf_op jit(solution)/shard_map/all_gather | solution.py:303
  10.0 591.8 %reduce-scatter.21.cloned.1.call-start = ((), (), s32[]{:S(2)}) async-start(), calls=%async_computation.15 | async-start | bytes 540672
  11.4 227.1 %collective-permute-start = (bf16[296,1024]{1,0:T(8,128)(2,1)S(1)}, bf16[296,1024]{1,0:T(8,128)(2,1)}, u32[]{:S(2)}, u32[]{:S(2)}) collective-permute-start(bf16[296,1024]{1,0:T(8,128)(2,1)S(1)} %select_bitcast_fusion.5), channel_id=1, source_target_pairs={{0,1},{1,0},{2,3},{3,2},{4,5},{5,4},{6,7},{7,6},{8,9},{9,8},{10,11... | collective-permute-start | bytes 1818632 | tf_op jit(solution)/shard_map/ppermute | solution.py:288
  15.4 225.5 %collective-permute-start.2 = (bf16[296,1024]{1,0:T(8,128)(2,1)}, bf16[296,1024]{1,0:T(8,128)(2,1)}, u32[]{:S(2)}, u32[]{:S(2)}) collective-permute-start(bf16[296,1024]{1,0:T(8,128)(2,1)} %select_bitcast_fusion.2), channel_id=1, source_target_pairs={{0,1},{1,0},{2,3},{3,2},{4,5},{5,4},{6,7},{7,6},{8,9},{9,8},{10,11... | collective-permute-start | bytes 1818632 | tf_op jit(solution)/shard_map/ppermute | solution.py:288
  239.7 0.8 copy-start.20
  240.9 34.0 %copy-start.2 = (bf16[592,1024]{1,0:T(8,128)(2,1)}, bf16[592,1024]{1,0:T(8,128)(2,1)S(1)}, u32[]{:S(2)}) copy-start(bf16[592,1024]{1,0:T(8,128)(2,1)S(1)} %fusion.36) | copy-start | bytes 3637252
  262.3 1.4 copy-start.22
  267.8 12.5 copy-start.6
  280.3 11.4 copy-start.28
  291.7 8.8 copy-start.30
  300.4 2.6 copy-start.25
  306.9 94.7 %copy-start.4 = (f32[592,1024]{1,0:T(8,128)}, f32[592,1024]{1,0:T(8,128)S(1)}, u32[]{:S(2)}) copy-start(f32[592,1024]{1,0:T(8,128)S(1)} %get-tuple-element.46) | copy-start | bytes 7274500
  332.2 30.2 %copy-start.8 = (bf16[8,4,1024,128]{3,0,2,1:T(8,128)(2,1)S(1)}, bf16[8,4,1024,128]{3,0,2,1:T(8,128)(2,1)}, u32[]{:S(2)}) copy-start(bf16[8,4,1024,128]{3,0,2,1:T(8,128)(2,1)} %copy.87) | copy-start | bytes 25165828
  332.2 30.2 %copy-start.36 = (f32[1,1024]{1,0:T(1,128)S(1)}, f32[1,1024]{1,0:T(1,128)}, u32[]{:S(2)}) copy-start(f32[1,1024]{1,0:T(1,128)} %get-tuple-element.36) | copy-start | bytes 12292
  362.5 5.4 copy-start.43
  367.8 1.1 copy-start.9
  367.9 1.2 copy-start.10
  367.9 1.2 copy-start.32
  368.3 1.9 copy-start.33
  372.7 18.2 %copy-start.16 = (f32[592,1024]{1,0:T(8,128)}, f32[592,1024]{1,0:T(8,128)S(1)}, u32[]{:S(2)}) copy-start(f32[592,1024]{1,0:T(8,128)S(1)} %get-tuple-element.18) | copy-start | bytes 7274500
  401.6 2.2 copy-start.21
  402.3 1.4 copy-start.18
  405.2 0.8 copy-start.31
  428.3 13.1 copy-start.15
  441.4 3.7 copy-start
  445.1 13.3 copy-start.11
  445.4 4.3 copy-start.26
  446.5 268.9 %reduce-scatter.19.cloned.1.call-start = ((), (), s32[]{:S(2)}) async-start(), calls=%async_computation.14 | async-start | bytes 540672
  449.6 404.9 %reduce-scatter.13.cloned.1.call-start = ((), (), s32[]{:S(2)}) async-start(), calls=%async_computation.7 | async-start | bytes 2162688 | tf_op jit(solution)/shard_map/reduce_scatter | solution.py:307
  453.2 1.8 copy-start.3
  454.7 518.0 %reduce-scatter.11.cloned.1.call-start = ((), (), s32[]{:S(2)}) async-start(), calls=%async_computation.6 | async-start | bytes 6488064 | tf_op jit(solution)/shard_map/reduce_scatter | solution.py:307
  458.5 1.5 copy-start.27
  459.9 3.3 copy-start.29
  459.9 3.3 copy-start.41
  463.2 1.3 copy-start.7
  475.2 1.7 copy-start.5
  475.3 684.4 %reduce-scatter.15.cloned.1.call-start = ((), (), s32[]{:S(2)}) async-start(), calls=%async_computation.8 | async-start | bytes 8650752 | tf_op jit(solution)/shard_map/reduce_scatter | solution.py:307
  513.4 1.7 copy-start.17
  513.4 831.9 %reduce-scatter.17.cloned.1.call-start = ((), (), s32[]{:S(2)}) async-start(), calls=%async_computation.9 | async-start | bytes 8650752 | tf_op jit(solution)/shard_map/reduce_scatter | solution.py:307
  551.1 1.3 copy-start.1
  553.3 163.5 %collective-permute-start.1 = (bf16[296,1024]{1,0:T(8,128)(2,1)}, bf16[296,1024]{1,0:T(8,128)(2,1)}, u32[]{:S(2)}, u32[]{:S(2)}) collective-permute-start(bf16[296,1024]{1,0:T(8,128)(2,1)} %broadcast_select_fusion.4), channel_id=1, source_target_pairs={{0,1},{1,0},{2,3},{3,2},{4,5},{5,4},{6,7},{7,6},{8,9},{9,8},{10,11... | collective-permute-start | bytes 1818632 | tf_op jit(solution)/shard_map/ppermute | solution.py:298
  553.3 3.0 copy-start.24
  553.3 3.0 copy-start.42
  556.3 1.3 copy-start.12
  556.3 2.1 copy-start.19
  556.3 2.7 copy-start.23
  559.1 4.5 copy-start.34
  561.5 157.6 %collective-permute-start.3 = (bf16[296,1024]{1,0:T(8,128)(2,1)}, bf16[296,1024]{1,0:T(8,128)(2,1)S(1)}, u32[]{:S(2)}, u32[]{:S(2)}) collective-permute-start(bf16[296,1024]{1,0:T(8,128)(2,1)} %broadcast_select_fusion.2), channel_id=1, source_target_pairs={{0,1},{1,0},{2,3},{3,2},{4,5},{5,4},{6,7},{7,6},{8,9},{9,8},{10,11... | collective-permute-start | bytes 1818632 | tf_op jit(solution)/shard_map/ppermute | solution.py:298
Sparse Core Ops, SparseCore 0:
  11.0 59.1 all-gather.13
  73.1 68.2 all-gather.11
  144.3 75.4 all-gather.15
  222.6 75.6 all-gather.17
  446.6 133.5 reduce-scatter.20
  582.9 132.4 reduce-scatter.18
  717.6 136.7 reduce-scatter.12
  860.1 112.5 reduce-scatter.10
  975.0 184.6 reduce-scatter.14
  1161.8 183.4 reduce-scatter.16
